TPU v7x, 32 devices: a whole 2x2x4 slice. The times are simulated.
32 devices in a mesh: layer: 4 (over y, x), row: 2 (over core), col: 4 (over z).
Axes of the slice: x: 2, y: 2, z: 4, core: 2. Of those that a mesh axis runs over, the one named last changes fastest.
Arguments:
- block_values: bfloat16 [4, 2, 4, 32, 256, 256], P('layer', 'row', 'col'), may hold values from 0 to 3
- block_rows: int32 [4, 2, 4, 32], P('layer', 'row', 'col'), may hold values from 0 to 255
- block_cols: int32 [4, 2, 4, 32], P('layer', 'row', 'col'), may hold values from 0 to 127
- block_count: int32 [4, 2, 4], P('layer', 'row', 'col'), may hold values from 1 to 32, as said below
- dangling: int32 [4, 2, 4, 16384], P('layer', 'row', 'col'), may hold values 0 or 1
- start_ranks: float32 [4, 2, 4, 16384], P('layer', 'row', 'col'), may hold values from 0.2 to 5
Outputs:
- ranks: float32 [4, 2, 4, 16384], P('layer', 'row', 'col')
- residuals: float32 [3, 4], P(None, 'layer')
Inputs may be any that keep to these rules, and one draw needn't show every extreme that they name: `block_count`: live slots of a tile; in every layer some tile has all 32 slots live. `block_rows`: slots at or past a tile's count carry no edges; coordinates may repeat within a tile, and repeated blocks add.
All inputs are finite; a program needn't handle non-finite values. No bound on the sum of `dangling` on one device may be relied on, other than what follows from the above.
Results may differ from a plain program's by a relative error of at most 0.0012.
Values may be sent and summed in bfloat16 or wider, within the bound.
A program may use at most 64 MiB of HBM per device.

v0:
```python
import jax
import jax.numpy as jnp
from jax import lax
from jax.sharding import PartitionSpec as P

ITERS = 3
damping = 0.85
coupling = 0.3


def with_halo(x, sides, width):
    for axis, dim in sides:
        count, length = (lax.axis_size(axis), x.shape[dim])
        up = [(i, (i + 1) % count) for i in range(count - 1)]
        down = [(j, i) for i, j in up]
        last = lax.slice_in_dim(x, length - width, length, axis=dim)
        first = lax.slice_in_dim(x, 0, width, axis=dim)
        before = lax.ppermute(last, axis, up)
        after = lax.ppermute(first, axis, down)
        x = jnp.concatenate([before, x, after], axis=dim)
    return x


def block_terms(values, rows_here, cols_here, live_here, column_bf, row_blk):
    picked = jnp.take(column_bf, cols_here, axis=0)
    products = jnp.einsum("sij,sj->si", values, picked, preferred_element_type=jnp.float32)
    onehot = (rows_here[:, None] == jnp.arange(row_blk)[None, :]).astype(jnp.float32) * live_here[
        :, None
    ]
    return jnp.einsum("sb,si->bi", onehot, products, precision=lax.Precision.HIGHEST)


def layer_walk(values, rows_here, cols_here, live_here, column_bf, row_blk):
    return block_terms(values, rows_here, cols_here, live_here, column_bf, row_blk)


def local(block_values, block_rows, block_cols, block_count, dangling, start_ranks):
    layer_dev = start_ranks.shape[0]
    span_len = start_ranks.shape[-1]
    row_devices = lax.axis_size("row")
    col_devices = lax.axis_size("col")
    block_edge = block_values.shape[-1]
    slots = block_values.shape[3]
    col_blk = row_devices * span_len // block_edge
    row_blk = col_devices * span_len // block_edge
    node_total = row_devices * col_devices * span_len
    layers = layer_dev * lax.axis_size("layer")
    values = block_values[:, 0, 0]
    block_row = block_rows[:, 0, 0]
    block_col = block_cols[:, 0, 0]
    counts = block_count[:, 0, 0]
    live_slot = (jnp.arange(slots)[None, :] < counts[:, None]).astype(jnp.float32)
    colsum = jnp.einsum(
        "lsij,i->lsj",
        values,
        jnp.ones((block_edge,), jnp.bfloat16),
        preferred_element_type=jnp.float32,
    )
    onehot = (block_col[..., None] == jnp.arange(col_blk)[None, None, :]).astype(
        jnp.float32
    ) * live_slot[..., None]
    deg_part = jnp.einsum("lsb,lsj->lbj", onehot, colsum, precision=lax.Precision.HIGHEST)
    deg_part = deg_part.reshape(layer_dev, row_devices, 1, span_len)
    degree = lax.psum(deg_part, "row")
    own_degree = lax.dynamic_slice_in_dim(degree, lax.axis_index("row"), 1, 1)
    keep_mask = 1.0 - dangling.astype(jnp.float32)
    own_denominator = keep_mask * own_degree + 1.0
    layer_ids = lax.axis_index("layer") * layer_dev + jnp.arange(layer_dev)
    spread = (
        jnp.where((layer_ids == 0) | (layer_ids == layers - 1), 1.0, 0.5).astype(jnp.float32)
        * coupling
    )
    spread = spread.reshape(layer_dev, 1, 1, 1)
    ranks_now = start_ranks
    residual_list = []
    for iteration in range(ITERS):
        spill = ranks_now * spread
        padded = with_halo(spill.astype(jnp.bfloat16), (("layer", 0),), 1).astype(spill.dtype)
        arrive = padded[:-2] + padded[2:]
        scaled_own = (ranks_now * keep_mask / own_denominator).astype(jnp.bfloat16)
        column_vec = lax.all_gather(scaled_own, "row", axis=1, tiled=True)
        dangle_mass = lax.psum(jnp.sum(ranks_now / own_denominator, axis=(1, 2, 3)), ("row", "col"))
        scaled = column_vec.reshape(layer_dev, col_blk, block_edge)
        layer_terms = [
            layer_walk(values[0], block_row[0], block_col[0], live_slot[0], scaled[0], row_blk)
        ]
        partial_value = jnp.stack(layer_terms).reshape(layer_dev, 1, col_devices, span_len)
        whole = lax.psum(partial_value, "col")
        walk_sum = lax.dynamic_slice_in_dim(whole, lax.axis_index("col"), 1, 2)
        updated = damping * (
            (1.0 - coupling) * (walk_sum + dangle_mass.reshape(layer_dev, 1, 1, 1) / node_total)
            + arrive
        ) + (1.0 - damping)
        change = jnp.sum(jnp.abs(updated - ranks_now), axis=(1, 2, 3))
        change_total = lax.psum(change, ("row", "col"))
        residual_list.append(change_total)
        ranks_now = updated
    return (ranks_now, jnp.stack(residual_list))


def solution(mesh):
    placed = (
        P("layer", "row", "col", None, None, None),
        P("layer", "row", "col", None),
        P("layer", "row", "col", None),
        P("layer", "row", "col"),
        P("layer", "row", "col", None),
        P("layer", "row", "col", None),
    )
    return jax.shard_map(
        local,
        mesh=mesh,
        in_specs=placed,
        out_specs=(P("layer", "row", "col", None), P(None, "layer")),
        check_vma=False,
    )
```

profile of v0, /device:TPU:1, one launch (start us, length us, event | category | flops | bytes accessed | tf_op | source)
XLA Modules:
  0.0 197.9 jit_solution(1086443442296965706)
XLA Ops:
  7.9 2.8 %fusion.6 = f32[1,32,256]{2,0,1:T(1,128)S(1)} fusion(bf16[1,1,1,32,256,256]{5,4,3,2,1,0:T(8,128)(2,1)} %param.8), kind=kOutput, calls=%fused_computation.9 | convolution fusion | flops 4194304 | bytes 4227072 | tf_op jit(solution)/shard_map/lsij,i->lsj/dot_general | solution.py:53
  12.1 20.4 %all-reduce.6.cloned.1.call-done = f32[1,2,1,16384]{3,2,0,1:T(1,128)} async-done(((f32[1,2,1,16384]{3,2,0,1:T(1,128)}), f32[1,2,1,16384]{3,2,0,1:T(1,128)}) %all-reduce.6.cloned.1.call-update) | async-done | bytes 131088 | tf_op jit(solution)/shard_map/psum | solution.py:64
  32.6 1.6 fusion.20
  34.3 1.9 all_gather.9
  37.3 3.4 %fusion.4 = f32[32,1,256]{2,1,0:T(1,128)S(1)} fusion(bf16[1,1,1,32,256,256]{5,4,3,2,1,0:T(8,128)(2,1)} %param.8, bf16[32,256,1]{1,0,2:T(8,128)(2,1)S(1)} %select_bitcast_fusion.2), kind=kOutput, calls=%fused_computation.7 | convolution fusion | flops 4194304 | bytes 4243456 | tf_op jit(solution)/shard_map/sij,sj->si/dot_general | solution.py:26
  42.2 3.4 %collective-permute-start = (bf16[1,1,1,16384]{3,2,0,1:T(2,128)(2,1)S(1)}, bf16[1,1,1,16384]{3,2,0,1:T(2,128)(2,1)S(1)}, u32[]{:S(2)}, u32[]{:S(2)}) collective-permute-start(bf16[1,1,1,16384]{3,2,0,1:T(2,128)(2,1)S(1)} %bitcast_convert_fusion), channel_id=1, source_target_pairs={{0,8},{8,16},{16,24},{1,9},{9,17},{17,25},{2,10},{10,18},{18,26},{... | collective-permute-start | bytes 98312 | tf_op jit(solution)/shard_map/ppermute | solution.py:18
  45.6 1.3 collective-permute-start.1
  46.9 17.9 %psum.72 = f32[1]{0:T(128)} all-reduce(f32[1]{0:T(128)} %bitcast.11), channel_id=1, replica_groups=mesh['layer'=4,'row'=2,'col'=4] {'row','col'}, use_global_device_ids=true, to_apply=%region_3.5 | all-reduce | flops 1 | bytes 8 | tf_op jit(solution)/shard_map/psum | solution.py:82
  65.4 11.0 %all-reduce.8.cloned.1.call-done = f32[1,1,4,16384]{3,2,0,1:T(4,128)} async-done(((f32[1,1,4,16384]{3,2,0,1:T(4,128)}), f32[1,1,4,16384]{3,2,0,1:T(4,128)}) %all-reduce.8.cloned.1.call-update) | async-done | bytes 262160 | tf_op jit(solution)/shard_map/psum | solution.py:88
  76.4 1.8 divide_reduce_fusion.1
  78.4 4.3 %all_gather.10 = bf16[1,2,1,16384]{3,2,0,1:T(2,128)(2,1)S(1)} all-gather(bf16[1,1,1,16384]{3,2,0,1:T(2,128)(2,1)S(1)} %get-tuple-element.22), channel_id=1, replica_groups=mesh['layer'=4,'row'=2,'col'=4] {'row'}, dimensions={1}, use_global_device_ids=true | all-gather | bytes 98304 | tf_op jit(solution)/shard_map/all_gather | solution.py:81
  83.9 3.4 %fusion.2 = f32[32,1,256]{2,1,0:T(1,128)S(1)} fusion(bf16[1,1,1,32,256,256]{5,4,3,2,1,0:T(8,128)(2,1)} %param.8, bf16[32,256,1]{1,0,2:T(8,128)(2,1)S(1)} %select_bitcast_fusion.1), kind=kOutput, calls=%fused_computation.5 | convolution fusion | flops 4194304 | bytes 4243456 | tf_op jit(solution)/shard_map/sij,sj->si/dot_general | solution.py:26
  88.6 3.1 %collective-permute-start.2 = (bf16[1,1,1,16384]{3,2,0,1:T(2,128)(2,1)S(1)}, bf16[1,1,1,16384]{3,2,0,1:T(2,128)(2,1)S(1)}, u32[]{:S(2)}, u32[]{:S(2)}) collective-permute-start(bf16[1,1,1,16384]{3,2,0,1:T(2,128)(2,1)S(1)} %get-tuple-element.23), channel_id=1, source_target_pairs={{0,8},{8,16},{16,24},{1,9},{9,17},{17,25},{2,10},{10,18},{18,26},{... | collective-permute-start | bytes 98312 | tf_op jit(solution)/shard_map/ppermute | solution.py:18
  93.0 17.0 %psum.74 = f32[1]{0:T(128)} all-reduce(f32[1]{0:T(128)} %bitcast.18), channel_id=1, replica_groups=mesh['layer'=4,'row'=2,'col'=4] {'row','col'}, use_global_device_ids=true, to_apply=%region_6.8 | all-reduce | flops 1 | bytes 8 | tf_op jit(solution)/shard_map/psum | solution.py:82
  110.7 11.1 %all-reduce.10.cloned.1.call-done = f32[1,1,4,16384]{3,2,0,1:T(4,128)} async-done(((f32[1,1,4,16384]{3,2,0,1:T(4,128)}), f32[1,1,4,16384]{3,2,0,1:T(4,128)}) %all-reduce.10.cloned.1.call-update) | async-done | bytes 262160 | tf_op jit(solution)/shard_map/psum | solution.py:88
  121.8 1.8 divide_reduce_fusion
  123.8 4.3 %all_gather.11 = bf16[1,2,1,16384]{3,2,0,1:T(2,128)(2,1)S(1)} all-gather(bf16[1,1,1,16384]{3,2,0,1:T(2,128)(2,1)S(1)} %get-tuple-element.20), channel_id=1, replica_groups=mesh['layer'=4,'row'=2,'col'=4] {'row'}, dimensions={1}, use_global_device_ids=true | all-gather | bytes 98304 | tf_op jit(solution)/shard_map/all_gather | solution.py:81
  129.3 3.4 %fusion = f32[32,1,256]{2,1,0:T(1,128)S(1)} fusion(bf16[1,1,1,32,256,256]{5,4,3,2,1,0:T(8,128)(2,1)} %param.8, bf16[32,256,1]{1,0,2:T(8,128)(2,1)S(1)} %select_bitcast_fusion), kind=kOutput, calls=%fused_computation.3 | convolution fusion | flops 4194304 | bytes 4243456 | tf_op jit(solution)/shard_map/sij,sj->si/dot_general | solution.py:26
  134.0 3.1 %collective-permute-start.4 = (bf16[1,1,1,16384]{3,2,0,1:T(2,128)(2,1)S(1)}, bf16[1,1,1,16384]{3,2,0,1:T(2,128)(2,1)S(1)}, u32[]{:S(2)}, u32[]{:S(2)}) collective-permute-start(bf16[1,1,1,16384]{3,2,0,1:T(2,128)(2,1)S(1)} %get-tuple-element.21), channel_id=1, source_target_pairs={{0,8},{8,16},{16,24},{1,9},{9,17},{17,25},{2,10},{10,18},{18,26},{... | collective-permute-start | bytes 98312 | tf_op jit(solution)/shard_map/ppermute | solution.py:18
  138.4 16.9 %psum.76 = f32[1]{0:T(128)} all-reduce(f32[1]{0:T(128)} %bitcast.23), channel_id=1, replica_groups=mesh['layer'=4,'row'=2,'col'=4] {'row','col'}, use_global_device_ids=true, to_apply=%region_9.11 | all-reduce | flops 1 | bytes 8 | tf_op jit(solution)/shard_map/psum | solution.py:82
  156.0 11.2 %all-reduce.12.cloned.1.call-done = f32[1,1,4,16384]{3,2,0,1:T(4,128)} async-done(((f32[1,1,4,16384]{3,2,0,1:T(4,128)}), f32[1,1,4,16384]{3,2,0,1:T(4,128)}) %all-reduce.12.cloned.1.call-update) | async-done | bytes 262160 | tf_op jit(solution)/shard_map/psum | solution.py:88
  167.2 2.6 %fusion.19 = (f32[]{:T(128)}, f32[]{:T(128)}, f32[]{:T(128)}, f32[1,1,1,16384]{3,2,0,1:T(1,128)}) fusion(f32[1,1,1,16384]{3,2,0,1:T(1,128)S(1)} %get-tuple-element.17, f32[1,1,1,16384]{3,2,1,0:T(1,128)S(1)} %copy-done.1, f32[1,1,1,16384]{3,2,0,1:T(1,128)S(1)} %get-tuple-element.15, bf16[1,1,1,16384]{3,2,0,1:T(2,128)(2,1)S(1)} %collective-permute-done.5, ...), kind=kLoop, calls=%fused_computation.43 | loop fusion | flops 344061 | bytes 426004 | tf_op jit(solution)/shard_map/reduce_sum | solution.py:94
  169.9 19.0 %all-reduce = (f32[1,1]{0,1:T(1,128)}, f32[1,1]{0,1:T(1,128)}, f32[1,1]{0,1:T(1,128)}) all-reduce(f32[1,1]{0,1:T(1,128)} %bitcast.29, f32[1,1]{0,1:T(1,128)} %bitcast.28, f32[1,1]{0,1:T(1,128)} %bitcast.27), channel_id=1, replica_groups=mesh['layer'=4,'row'=2,'col'=4] {'row','col'}, use_global_device_ids=true, to_apply=%region_15.17 | all-reduce | flops 3 | bytes 24 | tf_op jit(solution)/shard_map/psum | solution.py:95
  188.9 2.5 %pad_maximum_fusion.6 = f32[3,1]{0,1:T(1,128)} fusion(f32[1,1]{0,1:T(1,128)} %get-tuple-element.10, f32[1,1]{0,1:T(1,128)} %get-tuple-element.11, f32[1,1]{0,1:T(1,128)} %get-tuple-element.12), kind=kLoop, calls=%fused_computation.90 | loop fusion | flops 6 | bytes 24 | tf_op jit(solution)/shard_map/stack | solution.py:98
  (52 shorter events, 12.0 us)
Async XLA Ops:
  7.2 3.6 %copy-start.3 = (s32[1,1,1,32]{3,2,1,0:T(1,128)S(1)}, s32[1,1,1,32]{3,2,1,0:T(1,128)}, u32[]{:S(2)}) copy-start(s32[1,1,1,32]{3,2,1,0:T(1,128)} %param.10) | copy-start | bytes 388
  7.2 25.4 %copy-start = (s32[1,1,1,16384]{3,2,1,0:T(1,128)S(1)}, s32[1,1,1,16384]{3,2,1,0:T(1,128)}, u32[]{:S(2)}) copy-start(s32[1,1,1,16384]{3,2,1,0:T(1,128)} %param.12) | copy-start | bytes 196612
  7.2 25.4 %copy-start.1 = (f32[1,1,1,16384]{3,2,1,0:T(1,128)S(1)}, f32[1,1,1,16384]{3,2,1,0:T(1,128)}, u32[]{:S(2)}) copy-start(f32[1,1,1,16384]{3,2,1,0:T(1,128)} %param.13) | copy-start | bytes 196612
  7.2 25.4 %all-reduce.6.cloned.1.call-start = ((), (), s32[]{:S(2)}) async-start(), calls=%async_computation | async-start | bytes 262144 | tf_op jit(solution)/shard_map/psum | solution.py:64
  7.9 32.8 %copy-start.2 = (s32[1,1,1,32]{3,2,1,0:T(1,128)S(1)}, s32[1,1,1,32]{3,2,1,0:T(1,128)}, u32[]{:S(2)}) copy-start(s32[1,1,1,32]{3,2,1,0:T(1,128)} %param.9) | copy-start | bytes 388
  12.0 64.4 %all-reduce.8.cloned.1.call-start = ((), (), s32[]{:S(2)}) async-start(), calls=%async_computation.1 | async-start | bytes 524288 | tf_op jit(solution)/shard_map/psum | solution.py:88
  42.1 79.7 %all-reduce.10.cloned.1.call-start = ((), (), s32[]{:S(2)}) async-start(), calls=%async_computation.2 | async-start | bytes 524288 | tf_op jit(solution)/shard_map/psum | solution.py:88
  42.2 23.2 %collective-permute-start = (bf16[1,1,1,16384]{3,2,0,1:T(2,128)(2,1)S(1)}, bf16[1,1,1,16384]{3,2,0,1:T(2,128)(2,1)S(1)}, u32[]{:S(2)}, u32[]{:S(2)}) collective-permute-start(bf16[1,1,1,16384]{3,2,0,1:T(2,128)(2,1)S(1)} %bitcast_convert_fusion), channel_id=1, source_target_pairs={{0,8},{8,16},{16,24},{1,9},{9,17},{17,25},{2,10},{10,18},{18,26},{... | collective-permute-start | bytes 98312 | tf_op jit(solution)/shard_map/ppermute | solution.py:18
  45.6 19.8 %collective-permute-start.1 = (bf16[1,1,1,16384]{3,2,0,1:T(2,128)(2,1)S(1)}, bf16[1,1,1,16384]{3,2,0,1:T(2,128)(2,1)S(1)}, u32[]{:S(2)}, u32[]{:S(2)}) collective-permute-start(bf16[1,1,1,16384]{3,2,0,1:T(2,128)(2,1)S(1)} %bitcast_convert_fusion), channel_id=1, source_target_pairs={{8,0},{16,8},{24,16},{9,1},{17,9},{25,17},{10,2},{18,10},{26,18},{... | collective-permute-start | bytes 98312 | tf_op jit(solution)/shard_map/ppermute | solution.py:19
  88.6 78.6 %all-reduce.12.cloned.1.call-start = ((), (), s32[]{:S(2)}) async-start(), calls=%async_computation.3 | async-start | bytes 524288 | tf_op jit(solution)/shard_map/psum | solution.py:88
  88.6 22.1 %collective-permute-start.2 = (bf16[1,1,1,16384]{3,2,0,1:T(2,128)(2,1)S(1)}, bf16[1,1,1,16384]{3,2,0,1:T(2,128)(2,1)S(1)}, u32[]{:S(2)}, u32[]{:S(2)}) collective-permute-start(bf16[1,1,1,16384]{3,2,0,1:T(2,128)(2,1)S(1)} %get-tuple-element.23), channel_id=1, source_target_pairs={{0,8},{8,16},{16,24},{1,9},{9,17},{17,25},{2,10},{10,18},{18,26},{... | collective-permute-start | bytes 98312 | tf_op jit(solution)/shard_map/ppermute | solution.py:18
  91.7 19.0 %collective-permute-start.3 = (bf16[1,1,1,16384]{3,2,0,1:T(2,128)(2,1)S(1)}, bf16[1,1,1,16384]{3,2,0,1:T(2,128)(2,1)S(1)}, u32[]{:S(2)}, u32[]{:S(2)}) collective-permute-start(bf16[1,1,1,16384]{3,2,0,1:T(2,128)(2,1)S(1)} %get-tuple-element.23), channel_id=1, source_target_pairs={{8,0},{16,8},{24,16},{9,1},{17,9},{25,17},{10,2},{18,10},{26,18},{... | collective-permute-start | bytes 98312 | tf_op jit(solution)/shard_map/ppermute | solution.py:19
  134.0 22.0 %collective-permute-start.4 = (bf16[1,1,1,16384]{3,2,0,1:T(2,128)(2,1)S(1)}, bf16[1,1,1,16384]{3,2,0,1:T(2,128)(2,1)S(1)}, u32[]{:S(2)}, u32[]{:S(2)}) collective-permute-start(bf16[1,1,1,16384]{3,2,0,1:T(2,128)(2,1)S(1)} %get-tuple-element.21), channel_id=1, source_target_pairs={{0,8},{8,16},{16,24},{1,9},{9,17},{17,25},{2,10},{10,18},{18,26},{... | collective-permute-start | bytes 98312 | tf_op jit(solution)/shard_map/ppermute | solution.py:18
  137.1 18.9 %collective-permute-start.5 = (bf16[1,1,1,16384]{3,2,0,1:T(2,128)(2,1)S(1)}, bf16[1,1,1,16384]{3,2,0,1:T(2,128)(2,1)S(1)}, u32[]{:S(2)}, u32[]{:S(2)}) collective-permute-start(bf16[1,1,1,16384]{3,2,0,1:T(2,128)(2,1)S(1)} %get-tuple-element.21), channel_id=1, source_target_pairs={{8,0},{16,8},{24,16},{9,1},{17,9},{25,17},{10,2},{18,10},{26,18},{... | collective-permute-start | bytes 98312 | tf_op jit(solution)/shard_map/ppermute | solution.py:19
Sparse Core Ops, SparseCore 0:
  12.1 20.3 all-reduce.5
  42.2 34.1 all-reduce.7
  88.7 33.0 all-reduce.9
  134.1 33.0 all-reduce.11
where the time goes:
time: 199 us; the launch traced here: 198 us
  blocking collectives  81.3 us (41%)
  waiting for transfers between devices  53.8 us (27%)
  between operations  16.7 us (8%)
  matrix products  14.8 us (7%)
  starting transfers between devices  13.6 us (7%)
  other arithmetic  12.3 us (6%)
  local copies, waits for them, and re-layouts  5.32 us (3%)
    psum x3, blocking collectives, local(): lax.psum(jnp.sum(ranks_now / own_denominator, axis=(1, 2, 3)), ('row', 'c...  51.8 us
    psum x3, waiting for transfers between devices, local(): whole = lax.psum(partial_value, 'col')  33.3 us
    psum x1, waiting for transfers between devices, local(): degree = lax.psum(deg_part, 'row')  20.4 us
    psum x1, blocking collectives, local(): change_total = lax.psum(change, ('row', 'col'))  19 us
    all_gather x3, blocking collectives, local(): column_vec = lax.all_gather(scaled_own, 'row', axis=1, tiled=True)  10.5 us
    dot_general x3, matrix products, block_terms(): jnp.einsum('sij,sj->si', values, picked, preferred_element_type=jnp.float32)  10.1 us
    ppermute x3, starting transfers between devices, with_halo(): before = lax.ppermute(last, axis, up)  9.59 us
    reduce_sum x3, other arithmetic, local(): jnp.sum(ranks_now / own_denominator, axis=(1, 2, 3))  5.25 us
  transfers between devices with their start and end apart: 10, of which 4 were waited for; matrix products, arithmetic and copies ran while one was open for 0% of the time, Pallas kernels for 0%

commit v1 on v0

--- a/solution.py
+++ b/solution.py
@@ -85,7 +85,7 @@
             layer_walk(values[0], block_row[0], block_col[0], live_slot[0], scaled[0], row_blk)
         ]
         partial_value = jnp.stack(layer_terms).reshape(layer_dev, 1, col_devices, span_len)
-        whole = lax.psum(partial_value, "col")
+        whole = jnp.sum(lax.all_gather(partial_value, "col"), axis=0)
         walk_sum = lax.dynamic_slice_in_dim(whole, lax.axis_index("col"), 1, 2)
         updated = damping * (
             (1.0 - coupling) * (walk_sum + dangle_mass.reshape(layer_dev, 1, 1, 1) / node_total)

time: 199 us -> 178 us (0.89)
  waiting for transfers between devices: 53.8 us -> 35.2 us
  blocking collectives: 81.3 us -> 77.4 us
    psum x3 -> x0, waiting for transfers between devices: 33.3 us -> none  [local(): whole = lax.psum(partial_value, 'col')]
    all_gather x0 -> x3, waiting for transfers between devices: none -> 14.7 us  [local(): whole = jnp.sum(lax.all_gather(partial_value, 'col'), axis=0)]
    reduce_sum x0 -> x3, other arithmetic: none -> 4.4 us  [local(): whole = jnp.sum(lax.all_gather(partial_value, 'col'), axis=0)]
    all_gather x3, blocking collectives: 10.5 us -> 7.1 us  [local(): column_vec = lax.all_gather(scaled_own, 'row', axis=1, tiled=True)]
    psum x1, blocking collectives: 19 us -> 16.7 us  [local(): change_total = lax.psum(change, ('row', 'col'))]
  transfers between devices with their start and end apart: 10 -> 10, of which waited for: 4 -> 4; matrix products, arithmetic and copies ran while one was open for 0% -> 3% of each run, Pallas kernels for 0% -> 0%
where the time goes in v1:
time: 178 us; the launch traced here: 177 us
  blocking collectives  77.4 us (43%)
  waiting for transfers between devices  35.2 us (20%)
  between operations  16.7 us (9%)
  matrix products  14.8 us (8%)
  other arithmetic  13.9 us (8%)
  starting transfers between devices  13.7 us (8%)
  local copies, waits for them, and re-layouts  5.38 us (3%)
    psum x3, blocking collectives, local(): lax.psum(jnp.sum(ranks_now / own_denominator, axis=(1, 2, 3)), ('row', 'c...  53.7 us
    psum x1, waiting for transfers between devices, local(): degree = lax.psum(deg_part, 'row')  20.4 us
    psum x1, blocking collectives, local(): change_total = lax.psum(change, ('row', 'col'))  16.7 us
    all_gather x3, waiting for transfers between devices, local(): whole = jnp.sum(lax.all_gather(partial_value, 'col'), axis=0)  14.7 us
    dot_general x3, matrix products, block_terms(): jnp.einsum('sij,sj->si', values, picked, preferred_element_type=jnp.float32)  10.1 us
    ppermute x3, starting transfers between devices, with_halo(): before = lax.ppermute(last, axis, up)  9.67 us
    all_gather x3, blocking collectives, local(): column_vec = lax.all_gather(scaled_own, 'row', axis=1, tiled=True)  7.1 us
    reduce_sum x3, other arithmetic, local(): whole = jnp.sum(lax.all_gather(partial_value, 'col'), axis=0)  4.4 us
  transfers between devices with their start and end apart: 10, of which 4 were waited for; matrix products, arithmetic and copies ran while one was open for 3% of the time, Pallas kernels for 0%

profile of v1, /device:TPU:1, one launch (start us, length us, event | category | flops | bytes accessed | tf_op | source)
XLA Modules:
  0.0 177.1 jit_solution(1034075664587487139)
XLA Ops:
  7.9 2.8 %fusion.6 = f32[1,32,256]{2,0,1:T(1,128)S(1)} fusion(bf16[1,1,1,32,256,256]{5,4,3,2,1,0:T(8,128)(2,1)} %param.8), kind=kOutput, calls=%fused_computation.9 | convolution fusion | flops 4194304 | bytes 4227072 | tf_op jit(solution)/shard_map/lsij,i->lsj/dot_general | solution.py:53
  12.1 20.4 %all-reduce.3.cloned.1.call-done = f32[1,2,1,16384]{3,2,0,1:T(1,128)} async-done(((f32[1,2,1,16384]{3,2,0,1:T(1,128)}), f32[1,2,1,16384]{3,2,0,1:T(1,128)}) %all-reduce.3.cloned.1.call-update) | async-done | bytes 131088 | tf_op jit(solution)/shard_map/psum | solution.py:64
  32.6 1.6 fusion.20
  34.3 1.9 %all_gather.18 = bf16[1,2,1,16384]{3,2,0,1:T(2,128)(2,1)S(1)} all-gather(bf16[1,1,1,16384]{3,2,0,1:T(2,128)(2,1)S(1)} %fusion.23), channel_id=1, replica_groups=mesh['layer'=4,'row'=2,'col'=4] {'row'}, dimensions={1}, use_global_device_ids=true | all-gather | bytes 98304 | tf_op jit(solution)/shard_map/all_gather | solution.py:81
  37.3 3.4 %fusion.4 = f32[32,1,256]{2,1,0:T(1,128)S(1)} fusion(bf16[1,1,1,32,256,256]{5,4,3,2,1,0:T(8,128)(2,1)} %param.8, bf16[32,256,1]{1,0,2:T(8,128)(2,1)S(1)} %select_bitcast_fusion.2), kind=kOutput, calls=%fused_computation.7 | convolution fusion | flops 4194304 | bytes 4243456 | tf_op jit(solution)/shard_map/sij,sj->si/dot_general | solution.py:26
  42.2 3.4 %collective-permute-start = (bf16[1,1,1,16384]{3,2,0,1:T(2,128)(2,1)S(1)}, bf16[1,1,1,16384]{3,2,0,1:T(2,128)(2,1)S(1)}, u32[]{:S(2)}, u32[]{:S(2)}) collective-permute-start(bf16[1,1,1,16384]{3,2,0,1:T(2,128)(2,1)S(1)} %bitcast_convert_fusion), channel_id=1, source_target_pairs={{0,8},{8,16},{16,24},{1,9},{9,17},{17,25},{2,10},{10,18},{18,26},{... | collective-permute-start | bytes 98312 | tf_op jit(solution)/shard_map/ppermute | solution.py:18
  46.9 18.9 %psum.50 = f32[1]{0:T(128)} all-reduce(f32[1]{0:T(128)} %bitcast.10), channel_id=1, replica_groups=mesh['layer'=4,'row'=2,'col'=4] {'row','col'}, use_global_device_ids=true, to_apply=%region_3.5 | all-reduce | flops 1 | bytes 8 | tf_op jit(solution)/shard_map/psum | solution.py:82
  66.5 4.6 %all-gather.4.cloned.1.call-done = f32[4,1,1,4,16384]{4,3,2,1,0:T(4,128)} async-done(((f32[1,1,1,4,16384]{4,3,2,1,0:T(4,128)}), f32[4,1,1,4,16384]{4,3,2,1,0:T(4,128)}) %all-gather.4.cloned.1.call-update) | async-done | bytes 1048592 | tf_op jit(solution)/shard_map/all_gather | solution.py:88
  71.1 1.5 reduce_sum.93
  73.6 2.6 %all_gather.20 = bf16[1,2,1,16384]{3,2,0,1:T(2,128)(2,1)S(1)} all-gather(bf16[1,1,1,16384]{3,2,0,1:T(2,128)(2,1)S(1)} %get-tuple-element.22), channel_id=1, replica_groups=mesh['layer'=4,'row'=2,'col'=4] {'row'}, dimensions={1}, use_global_device_ids=true | all-gather | bytes 98304 | tf_op jit(solution)/shard_map/all_gather | solution.py:81
  77.4 3.4 %fusion.2 = f32[32,1,256]{2,1,0:T(1,128)S(1)} fusion(bf16[1,1,1,32,256,256]{5,4,3,2,1,0:T(8,128)(2,1)} %param.8, bf16[32,256,1]{1,0,2:T(8,128)(2,1)S(1)} %select_bitcast_fusion.1), kind=kOutput, calls=%fused_computation.5 | convolution fusion | flops 4194304 | bytes 4243456 | tf_op jit(solution)/shard_map/sij,sj->si/dot_general | solution.py:26
  82.2 3.3 %collective-permute-start.2 = (bf16[1,1,1,16384]{3,2,0,1:T(2,128)(2,1)S(1)}, bf16[1,1,1,16384]{3,2,0,1:T(2,128)(2,1)S(1)}, u32[]{:S(2)}, u32[]{:S(2)}) collective-permute-start(bf16[1,1,1,16384]{3,2,0,1:T(2,128)(2,1)S(1)} %get-tuple-element.23), channel_id=1, source_target_pairs={{0,8},{8,16},{16,24},{1,9},{9,17},{17,25},{2,10},{10,18},{18,26},{... | collective-permute-start | bytes 98312 | tf_op jit(solution)/shard_map/ppermute | solution.py:18
  86.8 17.4 %psum.51 = f32[1]{0:T(128)} all-reduce(f32[1]{0:T(128)} %bitcast.17), channel_id=1, replica_groups=mesh['layer'=4,'row'=2,'col'=4] {'row','col'}, use_global_device_ids=true, to_apply=%region_6.8 | all-reduce | flops 1 | bytes 8 | tf_op jit(solution)/shard_map/psum | solution.py:82
  104.9 4.9 %all-gather.6.cloned.1.call-done = f32[4,1,1,4,16384]{4,3,2,1,0:T(4,128)} async-done(((f32[1,1,1,4,16384]{4,3,2,1,0:T(4,128)}), f32[4,1,1,4,16384]{4,3,2,1,0:T(4,128)}) %all-gather.6.cloned.1.call-update) | async-done | bytes 1048592 | tf_op jit(solution)/shard_map/all_gather | solution.py:88
  109.7 1.5 reduce_sum.96
  112.2 2.6 %all_gather.22 = bf16[1,2,1,16384]{3,2,0,1:T(2,128)(2,1)S(1)} all-gather(bf16[1,1,1,16384]{3,2,0,1:T(2,128)(2,1)S(1)} %get-tuple-element.20), channel_id=1, replica_groups=mesh['layer'=4,'row'=2,'col'=4] {'row'}, dimensions={1}, use_global_device_ids=true | all-gather | bytes 98304 | tf_op jit(solution)/shard_map/all_gather | solution.py:81
  116.0 3.4 %fusion = f32[32,1,256]{2,1,0:T(1,128)S(1)} fusion(bf16[1,1,1,32,256,256]{5,4,3,2,1,0:T(8,128)(2,1)} %param.8, bf16[32,256,1]{1,0,2:T(8,128)(2,1)S(1)} %select_bitcast_fusion), kind=kOutput, calls=%fused_computation.3 | convolution fusion | flops 4194304 | bytes 4243456 | tf_op jit(solution)/shard_map/sij,sj->si/dot_general | solution.py:26
  120.8 3.0 %collective-permute-start.4 = (bf16[1,1,1,16384]{3,2,0,1:T(2,128)(2,1)S(1)}, bf16[1,1,1,16384]{3,2,0,1:T(2,128)(2,1)S(1)}, u32[]{:S(2)}, u32[]{:S(2)}) collective-permute-start(bf16[1,1,1,16384]{3,2,0,1:T(2,128)(2,1)S(1)} %get-tuple-element.21), channel_id=1, source_target_pairs={{0,8},{8,16},{16,24},{1,9},{9,17},{17,25},{2,10},{10,18},{18,26},{... | collective-permute-start | bytes 98312 | tf_op jit(solution)/shard_map/ppermute | solution.py:18
  125.1 17.3 %psum.52 = f32[1]{0:T(128)} all-reduce(f32[1]{0:T(128)} %bitcast.22), channel_id=1, replica_groups=mesh['layer'=4,'row'=2,'col'=4] {'row','col'}, use_global_device_ids=true, to_apply=%region_9.11 | all-reduce | flops 1 | bytes 8 | tf_op jit(solution)/shard_map/psum | solution.py:82
  143.1 5.2 %all-gather.8.cloned.1.call-done = f32[4,1,1,4,16384]{4,3,2,1,0:T(4,128)} async-done(((f32[1,1,1,4,16384]{4,3,2,1,0:T(4,128)}), f32[4,1,1,4,16384]{4,3,2,1,0:T(4,128)}) %all-gather.8.cloned.1.call-update) | async-done | bytes 1048592 | tf_op jit(solution)/shard_map/all_gather | solution.py:88
  148.2 1.5 reduce_sum.99
  149.7 1.7 fusion.19
  151.4 16.7 %all-reduce = (f32[1,1]{0,1:T(1,128)}, f32[1,1]{0,1:T(1,128)}, f32[1,1]{0,1:T(1,128)}) all-reduce(f32[1,1]{0,1:T(1,128)} %bitcast.29, f32[1,1]{0,1:T(1,128)} %bitcast.28, f32[1,1]{0,1:T(1,128)} %bitcast.27), channel_id=1, replica_groups=mesh['layer'=4,'row'=2,'col'=4] {'row','col'}, use_global_device_ids=true, to_apply=%region_15.17 | all-reduce | flops 3 | bytes 24 | tf_op jit(solution)/shard_map/psum | solution.py:95
  168.1 2.4 %pad_maximum_fusion.6 = f32[3,1]{0,1:T(1,128)} fusion(f32[1,1]{0,1:T(1,128)} %get-tuple-element.10, f32[1,1]{0,1:T(1,128)} %get-tuple-element.11, f32[1,1]{0,1:T(1,128)} %get-tuple-element.12), kind=kLoop, calls=%fused_computation.90 | loop fusion | flops 6 | bytes 24 | tf_op jit(solution)/shard_map/stack | solution.py:98
  (55 shorter events, 15.1 us)
Async XLA Ops:
  7.2 3.6 %copy-start.3 = (s32[1,1,1,32]{3,2,1,0:T(1,128)S(1)}, s32[1,1,1,32]{3,2,1,0:T(1,128)}, u32[]{:S(2)}) copy-start(s32[1,1,1,32]{3,2,1,0:T(1,128)} %param.10) | copy-start | bytes 388
  7.2 25.4 %copy-start = (s32[1,1,1,16384]{3,2,1,0:T(1,128)S(1)}, s32[1,1,1,16384]{3,2,1,0:T(1,128)}, u32[]{:S(2)}) copy-start(s32[1,1,1,16384]{3,2,1,0:T(1,128)} %param.12) | copy-start | bytes 196612
  7.2 25.4 %copy-start.1 = (f32[1,1,1,16384]{3,2,1,0:T(1,128)S(1)}, f32[1,1,1,16384]{3,2,1,0:T(1,128)}, u32[]{:S(2)}) copy-start(f32[1,1,1,16384]{3,2,1,0:T(1,128)} %param.13) | copy-start | bytes 196612
  7.2 25.4 %all-reduce.3.cloned.1.call-start = ((), (), s32[]{:S(2)}) async-start(), calls=%async_computation | async-start | bytes 262144 | tf_op jit(solution)/shard_map/psum | solution.py:64
  7.9 32.8 %copy-start.2 = (s32[1,1,1,32]{3,2,1,0:T(1,128)S(1)}, s32[1,1,1,32]{3,2,1,0:T(1,128)}, u32[]{:S(2)}) copy-start(s32[1,1,1,32]{3,2,1,0:T(1,128)} %param.9) | copy-start | bytes 388
  12.0 59.1 %all-gather.4.cloned.1.call-start = ((), (), s32[]{:S(2)}) async-start(), calls=%async_computation.1 | async-start | bytes 1310720 | tf_op jit(solution)/shard_map/all_gather | solution.py:88
  42.1 67.6 %all-gather.6.cloned.1.call-start = ((), (), s32[]{:S(2)}) async-start(), calls=%async_computation.2 | async-start | bytes 1310720 | tf_op jit(solution)/shard_map/all_gather | solution.py:88
  42.2 30.3 %collective-permute-start = (bf16[1,1,1,16384]{3,2,0,1:T(2,128)(2,1)S(1)}, bf16[1,1,1,16384]{3,2,0,1:T(2,128)(2,1)S(1)}, u32[]{:S(2)}, u32[]{:S(2)}) collective-permute-start(bf16[1,1,1,16384]{3,2,0,1:T(2,128)(2,1)S(1)} %bitcast_convert_fusion), channel_id=1, source_target_pairs={{0,8},{8,16},{16,24},{1,9},{9,17},{17,25},{2,10},{10,18},{18,26},{... | collective-permute-start | bytes 98312 | tf_op jit(solution)/shard_map/ppermute | solution.py:18
  45.6 27.0 %collective-permute-start.1 = (bf16[1,1,1,16384]{3,2,0,1:T(2,128)(2,1)S(1)}, bf16[1,1,1,16384]{3,2,0,1:T(2,128)(2,1)S(1)}, u32[]{:S(2)}, u32[]{:S(2)}) collective-permute-start(bf16[1,1,1,16384]{3,2,0,1:T(2,128)(2,1)S(1)} %bitcast_convert_fusion), channel_id=1, source_target_pairs={{8,0},{16,8},{24,16},{9,1},{17,9},{25,17},{10,2},{18,10},{26,18},{... | collective-permute-start | bytes 98312 | tf_op jit(solution)/shard_map/ppermute | solution.py:19
  82.1 66.1 %all-gather.8.cloned.1.call-start = ((), (), s32[]{:S(2)}) async-start(), calls=%async_computation.3 | async-start | bytes 1310720 | tf_op jit(solution)/shard_map/all_gather | solution.py:88
  82.2 29.0 %collective-permute-start.2 = (bf16[1,1,1,16384]{3,2,0,1:T(2,128)(2,1)S(1)}, bf16[1,1,1,16384]{3,2,0,1:T(2,128)(2,1)S(1)}, u32[]{:S(2)}, u32[]{:S(2)}) collective-permute-start(bf16[1,1,1,16384]{3,2,0,1:T(2,128)(2,1)S(1)} %get-tuple-element.23), channel_id=1, source_target_pairs={{0,8},{8,16},{16,24},{1,9},{9,17},{17,25},{2,10},{10,18},{18,26},{... | collective-permute-start | bytes 98312 | tf_op jit(solution)/shard_map/ppermute | solution.py:18
  85.5 25.7 %collective-permute-start.3 = (bf16[1,1,1,16384]{3,2,0,1:T(2,128)(2,1)S(1)}, bf16[1,1,1,16384]{3,2,0,1:T(2,128)(2,1)S(1)}, u32[]{:S(2)}, u32[]{:S(2)}) collective-permute-start(bf16[1,1,1,16384]{3,2,0,1:T(2,128)(2,1)S(1)} %get-tuple-element.23), channel_id=1, source_target_pairs={{8,0},{16,8},{24,16},{9,1},{17,9},{25,17},{10,2},{18,10},{26,18},{... | collective-permute-start | bytes 98312 | tf_op jit(solution)/shard_map/ppermute | solution.py:19
  120.8 28.9 %collective-permute-start.4 = (bf16[1,1,1,16384]{3,2,0,1:T(2,128)(2,1)S(1)}, bf16[1,1,1,16384]{3,2,0,1:T(2,128)(2,1)S(1)}, u32[]{:S(2)}, u32[]{:S(2)}) collective-permute-start(bf16[1,1,1,16384]{3,2,0,1:T(2,128)(2,1)S(1)} %get-tuple-element.21), channel_id=1, source_target_pairs={{0,8},{8,16},{16,24},{1,9},{9,17},{17,25},{2,10},{10,18},{18,26},{... | collective-permute-start | bytes 98312 | tf_op jit(solution)/shard_map/ppermute | solution.py:18
  123.8 26.0 %collective-permute-start.5 = (bf16[1,1,1,16384]{3,2,0,1:T(2,128)(2,1)S(1)}, bf16[1,1,1,16384]{3,2,0,1:T(2,128)(2,1)S(1)}, u32[]{:S(2)}, u32[]{:S(2)}) collective-permute-start(bf16[1,1,1,16384]{3,2,0,1:T(2,128)(2,1)S(1)} %get-tuple-element.21), channel_id=1, source_target_pairs={{8,0},{16,8},{24,16},{9,1},{17,9},{25,17},{10,2},{18,10},{26,18},{... | collective-permute-start | bytes 98312 | tf_op jit(solution)/shard_map/ppermute | solution.py:19
Sparse Core Ops, SparseCore 0:
  12.1 20.3 all-reduce.2
  42.2 28.8 all-gather.3
  82.3 27.4 all-gather.5
  120.9 27.2 all-gather.7
